TPU v7x, 32 devices: a whole 2x2x4 slice. The times are simulated.
32 devices in a mesh: row: 4 (over z), col: 8 (over y, x, core).
Axes of the slice: x: 2, y: 2, z: 4, core: 2. Of those that a mesh axis runs over, the one named last changes fastest.
Arguments:
- node_latent: bfloat16 [32768, 128], P(('row', 'col')), may hold values from -6 to 6
- edge_latent: bfloat16 [131072, 128], P(('row', 'col')), may hold values from -6 to 6
- senders: int32 [131072], P(('row', 'col')), may hold values from 0 to 1535
- receivers: int32 [131072], P(('row', 'col')), may hold values from 0 to 1023
- send_index: int32 [32, 4, 128], P(('row', 'col')), may hold values from 0 to 1023
- context_table: bfloat16 [256, 128], P(('row', 'col')), may hold values from -6 to 6
- region: int32 [32768], P(('row', 'col')), may hold values from 0 to 255
- edge_w1: bfloat16 [2, 384, 128], replicated, may hold values from -0.3125 to 0.3125
- edge_w2: bfloat16 [2, 128, 128], replicated, may hold values from -0.5 to 0.5
- edge_bias: float32 [2, 3, 128], replicated, may hold values from -3 to 3
- edge_gain: float32 [2, 128], replicated, may hold values from 0.25 to 1.75
- node_w1: bfloat16 [2, 384, 128], replicated, may hold values from -0.3125 to 0.3125
- node_wg: bfloat16 [2, 128, 128], replicated, may hold values from -0.5 to 0.5
- node_w2: bfloat16 [2, 128, 128], replicated, may hold values from -0.5 to 0.5
- node_bias: float32 [2, 3, 128], replicated, may hold values from -3 to 3
- node_gain: float32 [2, 128], replicated, may hold values from 0.25 to 1.75
Outputs:
- node_out: bfloat16 [32768, 128], P(('row', 'col'))
- edge_out: bfloat16 [131072, 128], P(('row', 'col'))
Inputs may be any that keep to these rules, and one draw needn't show every extreme that they name: senders index the extended table of the edge's own partition: below 1024 its own nodes, then the four received blocks of 128 rows in the order above, below, left, right. receivers are nodes of the edge's own partition. `send_index`: rows of the sending partition's own nodes; repeats may occur.
All inputs are finite; a program needn't handle non-finite values.
Results may differ from a plain program's by a relative error of at most 0.0085.
Values may be sent and summed in bfloat16 or wider, within the bound.
A program may use at most 64 MiB of HBM per device.

v0:
```python
import math
import jax
import jax.numpy as jnp
from jax import lax
from jax.sharding import PartitionSpec as P

LAYERS = 2
EPS = 1e-05


def passed_along(value, axis, by):
    devices = lax.axis_size(axis)
    pairs = [(i, i + by) for i in range(devices) if 0 <= i + by < devices]
    return lax.ppermute(value, axis, pairs)


def norm_tail(pre, w_out, b_out, gain, shift):
    hidden = jax.nn.relu(pre).astype(jnp.bfloat16)
    y_val = jnp.dot(hidden, w_out, preferred_element_type=jnp.float32) + b_out
    centred = y_val - jnp.mean(y_val, axis=-1, keepdims=True)
    spread = jnp.mean(centred * centred, axis=-1, keepdims=True)
    return centred * lax.rsqrt(spread + EPS) * gain + shift


def one_hot(index, count):
    columns = lax.broadcasted_iota(jnp.int32, (1, count), 1)
    return (index[:, None] == columns).astype(jnp.bfloat16)


def lookup(index, table):
    picker = one_hot(index, table.shape[0])
    return jnp.dot(picker, table, preferred_element_type=jnp.float32).astype(jnp.bfloat16)


def blocked_lookup(index, table):
    total_rows = index.shape[0]
    block_rows = math.gcd(total_rows, 512)
    pieces = index.reshape(total_rows // block_rows, block_rows)
    result = lax.map(lambda piece: lookup(piece, table), pieces)
    return result.reshape(total_rows, table.shape[1])


def edge_and_sum(extended, nodes, edges, senders, receivers, w_in, w_out, bias, gain):
    total_rows = edges.shape[0]
    width = edges.shape[1]
    node_count = nodes.shape[0]
    block_rows = math.gcd(total_rows, 512)
    blocks = total_rows // block_rows

    def one_block(summed, items):
        edge_rows, send_rows, recv_rows = items
        recv_hot = one_hot(recv_rows, node_count)
        sender_feats = lookup(send_rows, extended)
        receiver_feats = jnp.dot(recv_hot, nodes, preferred_element_type=jnp.float32).astype(
            jnp.bfloat16
        )
        feats = jnp.concatenate([sender_feats, receiver_feats, edge_rows], axis=1)
        pre = jnp.dot(feats, w_in, preferred_element_type=jnp.float32) + bias[0]
        fresh = (
            edge_rows.astype(jnp.float32) + norm_tail(pre, w_out, bias[1], gain, bias[2])
        ).astype(jnp.bfloat16)
        added = lax.dot_general(
            recv_hot, fresh, (((0,), (0,)), ((), ())), preferred_element_type=jnp.float32
        )
        return (summed + added, fresh)

    start = jnp.zeros((node_count, width), jnp.float32)
    items = (
        edges.reshape(blocks, block_rows, width),
        senders.reshape(blocks, block_rows),
        receivers.reshape(blocks, block_rows),
    )
    summed, fresh = lax.scan(one_block, start, items)
    return (fresh.reshape(total_rows, width), summed.astype(jnp.bfloat16))


def node_step(nodes, summed, context_rows, w_in, w_out, bias, gain, shift_in):
    feats = jnp.concatenate([nodes, summed, context_rows], axis=1)
    pre = jnp.dot(feats, w_in, preferred_element_type=jnp.float32) + shift_in
    return (nodes.astype(jnp.float32) + norm_tail(pre, w_out, bias[1], gain, bias[2])).astype(
        jnp.bfloat16
    )


def row_move(block, offset):
    return passed_along(block, "row", offset)


def col_move(block, offset):
    return passed_along(block, "col", offset)


def extend(nodes, send_index):
    count = send_index.shape[2]
    width = nodes.shape[1]
    picked = lookup(send_index.reshape(-1), nodes).reshape(4, count, width)
    return jnp.concatenate(
        [
            nodes,
            row_move(picked[0], 1),
            row_move(picked[1], -1),
            col_move(picked[2], 1),
            col_move(picked[3], -1),
        ],
        axis=0,
    )


def local(
    node_latent,
    edge_latent,
    senders,
    receivers,
    send_index,
    context_table,
    region,
    edge_w1,
    edge_w2,
    edge_bias,
    edge_gain,
    node_w1,
    node_wg,
    node_w2,
    node_bias,
    node_gain,
):
    width = node_latent.shape[1]
    local_sum = jnp.sum(node_latent.astype(jnp.float32), axis=0)
    total = lax.psum(local_sum, ("row", "col"))
    by_row = lax.all_gather(context_table[None], "row", axis=0, tiled=True)
    table = lax.all_gather(by_row, "col", axis=1, tiled=True).reshape(-1, width)
    node_count = node_latent.shape[0] * lax.axis_size("row") * lax.axis_size("col")
    pooled = total / math.sqrt(node_count)
    context_rows = blocked_lookup(region, table)
    nodes = node_latent
    edges = edge_latent
    for layer in range(LAYERS):
        extended = extend(nodes, send_index)
        edges, summed = edge_and_sum(
            extended,
            nodes,
            edges,
            senders,
            receivers,
            edge_w1[layer],
            edge_w2[layer],
            edge_bias[layer],
            edge_gain[layer],
        )
        shift_in = node_bias[layer, 0] + jnp.dot(
            pooled, node_wg[layer].astype(jnp.float32), precision=lax.Precision.HIGHEST
        )
        nodes = node_step(
            nodes,
            summed,
            context_rows,
            node_w1[layer],
            node_w2[layer],
            node_bias[layer],
            node_gain[layer],
            shift_in,
        )
    return (nodes, edges)


def solution(mesh):
    return jax.shard_map(
        local,
        mesh=mesh,
        in_specs=(
            P(("row", "col"), None),
            P(("row", "col"), None),
            P(("row", "col")),
            P(("row", "col")),
            P(("row", "col"), None, None),
            P(("row", "col"), None),
            P(("row", "col")),
            P(),
            P(),
            P(),
            P(),
            P(),
            P(),
            P(),
            P(),
            P(),
        ),
        out_specs=(P(("row", "col"), None), P(("row", "col"), None)),
        check_vma=False,
    )
```

profile of v0, /device:TPU:11, one launch (start us, length us, event | category | flops | bytes accessed | tf_op | source)
XLA Modules:
  0.0 200.9 jit_solution(13532602859649688257)
XLA Ops:
  0.7 1.5 fusion.61
  2.9 3.2 %collective-permute-start = (bf16[128,128]{1,0:T(8,128)(2,1)}, bf16[128,128]{1,0:T(8,128)(2,1)S(1)}, u32[]{:S(2)}, u32[]{:S(2)}) collective-permute-start(bf16[128,128]{1,0:T(8,128)(2,1)} %get-tuple-element.356), channel_id=1, source_target_pairs={{0,8},{8,16},{16,24},{1,9},{9,17},{17,25},{2,10},{10,18},{18,26},{... | collective-permute-start | bytes 98312 | tf_op jit(solution)/shard_map/ppermute | solution.py:14
  6.1 2.1 %collective-permute-start.1 = (bf16[128,128]{1,0:T(8,128)(2,1)}, bf16[128,128]{1,0:T(8,128)(2,1)S(1)}, u32[]{:S(2)}, u32[]{:S(2)}) collective-permute-start(bf16[128,128]{1,0:T(8,128)(2,1)} %get-tuple-element.355), channel_id=1, source_target_pairs={{8,0},{16,8},{24,16},{9,1},{17,9},{25,17},{10,2},{18,10},{26,18},{... | collective-permute-start | bytes 98312 | tf_op jit(solution)/shard_map/ppermute | solution.py:14
  8.2 4.2 %collective-permute-start.2 = (bf16[128,128]{1,0:T(8,128)(2,1)S(1)}, bf16[128,128]{1,0:T(8,128)(2,1)S(1)}, u32[]{:S(2)}, u32[]{:S(2)}) collective-permute-start(bf16[128,128]{1,0:T(8,128)(2,1)S(1)} %get-tuple-element.354), channel_id=1, source_target_pairs={{0,1},{1,2},{2,3},{3,4},{4,5},{5,6},{6,7},{8,9},{9,10},{10,11},{11... | collective-permute-start | bytes 98312 | tf_op jit(solution)/shard_map/ppermute | solution.py:14
  12.4 1.9 collective-permute-start.3
  15.4 40.4 %psum.7 = f32[128]{0:T(128)S(1)} all-reduce(f32[128]{0:T(128)S(1)} %convert_reduce_fusion), channel_id=1, replica_groups=mesh['row'=4,'col'=8] {'row','col'}, use_global_device_ids=true, to_apply=%region_7.8 | all-reduce | flops 128 | bytes 1024 | tf_op jit(solution)/shard_map/psum | solution.py:129
  56.3 8.2 %all-gather = bf16[32,128]{1,0:T(8,128)(2,1)S(1)} all-gather(bf16[8,128]{1,0:T(8,128)(2,1)S(1)} %copy-done.10), channel_id=2, replica_groups=mesh['row'=4,'col'=8] {'row'}, dimensions={0}, use_global_device_ids=true | all-gather | bytes 10240 | tf_op jit(solution)/shard_map/all_gather | solution.py:130
  64.5 12.8 %all_gather.7 = bf16[4,64,128]{2,1,0:T(8,128)(2,1)S(1)} all-gather(bf16[4,8,128]{2,1,0:T(8,128)(2,1)S(1)} %bitcast.189), channel_id=1, replica_groups=mesh['row'=4,'col'=8] {'col'}, dimensions={1}, use_global_device_ids=true | all-gather | bytes 73728 | tf_op jit(solution)/shard_map/all_gather | solution.py:131
  79.1 50.7 %while.37 = (s32[]{:T(128)}, f32[1024,128]{1,0:T(8,128)S(1)}, bf16[8,512,128]{1,2,0:T(8,128)(2,1)S(1)}, s32[8,512]{1,0:T(8,128)S(1)}, bf16[8,512,128]{2,1,0:T(8,...) while((s32[]{:T(128)}, f32[1024,128]{1,0:T(8,128)S(1)}, ...), condition=%wide.region_3.4_spmd.clone, body=%wide.region_0.3_spmd.clone.sunk | while | flops 541786624 | bytes 4363419 | solution.py:73
  80.4 1.5 fusion.176
  86.7 1.5 fusion.176
  93.1 1.5 fusion.176
  99.4 1.5 fusion.176
  105.7 1.5 fusion.176
  112.0 1.5 fusion.176
  118.4 1.5 fusion.176
  124.7 1.5 fusion.176
  129.9 1.5 fusion.125
  132.8 2.8 %collective-permute-start.4 = (bf16[128,128]{0,1:T(8,128)(2,1)S(1)}, bf16[128,128]{0,1:T(8,128)(2,1)S(1)}, u32[]{:S(2)}, u32[]{:S(2)}) collective-permute-start(bf16[128,128]{0,1:T(8,128)(2,1)S(1)} %get-tuple-element.352), channel_id=1, source_target_pairs={{0,8},{8,16},{16,24},{1,9},{9,17},{17,25},{2,10},{10,18},{18,26},{... | collective-permute-start | bytes 98312 | tf_op jit(solution)/shard_map/ppermute | solution.py:14
  136.5 2.5 %collective-permute-start.5 = (bf16[128,128]{0,1:T(8,128)(2,1)S(1)}, bf16[128,128]{0,1:T(8,128)(2,1)S(1)}, u32[]{:S(2)}, u32[]{:S(2)}) collective-permute-start(bf16[128,128]{0,1:T(8,128)(2,1)S(1)} %get-tuple-element.351), channel_id=1, source_target_pairs={{8,0},{16,8},{24,16},{9,1},{17,9},{25,17},{10,2},{18,10},{26,18},{... | collective-permute-start | bytes 98312 | tf_op jit(solution)/shard_map/ppermute | solution.py:14
  139.1 3.7 %collective-permute-start.6 = (bf16[128,128]{0,1:T(8,128)(2,1)S(1)}, bf16[128,128]{0,1:T(8,128)(2,1)S(1)}, u32[]{:S(2)}, u32[]{:S(2)}) collective-permute-start(bf16[128,128]{0,1:T(8,128)(2,1)S(1)} %get-tuple-element.350), channel_id=1, source_target_pairs={{0,1},{1,2},{2,3},{3,4},{4,5},{5,6},{6,7},{8,9},{9,10},{10,11},{11... | collective-permute-start | bytes 98312 | tf_op jit(solution)/shard_map/ppermute | solution.py:14
  142.8 1.9 collective-permute-start.7
  144.8 4.1 %collective-permute-done.7 = bf16[128,128]{0,1:T(8,128)(2,1)S(1)} collective-permute-done((bf16[128,128]{0,1:T(8,128)(2,1)S(1)}, bf16[128,128]{0,1:T(8,128)(2,1)S(1)}, u32[]{:S(2)}, u32[]{:S(2)}) %collective-permute-start.7) | collective-permute-done | bytes 32800 | tf_op jit(solution)/shard_map/ppermute | solution.py:14
  149.2 49.0 %while.38 = (s32[]{:T(128)}, f32[1024,128]{1,0:T(8,128)S(1)}, bf16[8,512,128]{2,1,0:T(8,128)(2,1)}, s32[8,512]{1,0:T(8,128)S(1)}, bf16[8,512,128]{1,2,0:T(8,128)...) while((s32[]{:T(128)}, f32[1024,128]{1,0:T(8,128)S(1)}, ...), condition=%wide.region_13.14_spmd.clone, body=%wide.region_10.13_spmd.clone.sunk | while | flops 541786624 | bytes 4495003 | solution.py:73
  150.5 1.5 fusion.186
  156.6 1.5 fusion.186
  162.7 1.5 fusion.186
  168.8 1.5 fusion.186
  175.0 1.5 fusion.186
  181.1 1.5 fusion.186
  187.2 1.5 fusion.186
  193.3 1.5 fusion.186
  (281 shorter events, 84.0 us)
Async XLA Ops:
  0.6 13.7 %copy-start = (bf16[1024,128]{1,0:T(8,128)(2,1)S(1)}, bf16[1024,128]{1,0:T(8,128)(2,1)}, u32[]{:S(2)}) copy-start(bf16[1024,128]{1,0:T(8,128)(2,1)} %param.22) | copy-start | bytes 786436
  0.6 13.9 %copy-start.1 = (bf16[2,384,128]{2,1,0:T(8,128)(2,1)S(1)}, bf16[2,384,128]{2,1,0:T(8,128)(2,1)}, u32[]{:S(2)}) copy-start(bf16[2,384,128]{2,1,0:T(8,128)(2,1)} %param.29) | copy-start | bytes 589828
  0.7 13.9 %copy-start.2 = (bf16[2,128,128]{2,1,0:T(8,128)(2,1)S(1)}, bf16[2,128,128]{2,1,0:T(8,128)(2,1)}, u32[]{:S(2)}) copy-start(bf16[2,128,128]{2,1,0:T(8,128)(2,1)} %param.30) | copy-start | bytes 196612
  0.7 14.5 %copy-start.7 = (f32[2,3,128]{2,0,1:T(2,128)S(1)}, f32[2,3,128]{2,0,1:T(2,128)}, u32[]{:S(2)}) copy-start(f32[2,3,128]{2,0,1:T(2,128)} %param.31) | copy-start | bytes 9220
  0.7 14.5 %copy-start.12 = (f32[2,128]{1,0:T(2,128)S(1)}, f32[2,128]{1,0:T(2,128)}, u32[]{:S(2)}) copy-start(f32[2,128]{1,0:T(2,128)} %param.32) | copy-start | bytes 3076
  2.2 53.5 %copy-start.11 = (f32[2,3,128]{2,0,1:T(2,128)S(1)}, f32[2,3,128]{2,0,1:T(2,128)}, u32[]{:S(2)}) copy-start(f32[2,3,128]{2,0,1:T(2,128)} %param.36) | copy-start | bytes 9220
  2.2 54.1 %copy-start.10 = (bf16[8,128]{1,0:T(8,128)(2,1)S(1)}, bf16[8,128]{1,0:T(8,128)(2,1)}, u32[]{:S(2)}) copy-start(bf16[8,128]{1,0:T(8,128)(2,1)} %param.27) | copy-start | bytes 6148
  2.2 75.0 %copy-start.6 = (s32[1024]{0:T(1024)S(1)}, s32[1024]{0:T(1024)}, u32[]{:S(2)}) copy-start(s32[1024]{0:T(1024)} %param.28) | copy-start | bytes 12292
  2.9 76.1 %collective-permute-start = (bf16[128,128]{1,0:T(8,128)(2,1)}, bf16[128,128]{1,0:T(8,128)(2,1)S(1)}, u32[]{:S(2)}, u32[]{:S(2)}) collective-permute-start(bf16[128,128]{1,0:T(8,128)(2,1)} %get-tuple-element.356), channel_id=1, source_target_pairs={{0,8},{8,16},{16,24},{1,9},{9,17},{17,25},{2,10},{10,18},{18,26},{... | collective-permute-start | bytes 98312 | tf_op jit(solution)/shard_map/ppermute | solution.py:14
  6.1 72.9 %collective-permute-start.1 = (bf16[128,128]{1,0:T(8,128)(2,1)}, bf16[128,128]{1,0:T(8,128)(2,1)S(1)}, u32[]{:S(2)}, u32[]{:S(2)}) collective-permute-start(bf16[128,128]{1,0:T(8,128)(2,1)} %get-tuple-element.355), channel_id=1, source_target_pairs={{8,0},{16,8},{24,16},{9,1},{17,9},{25,17},{10,2},{18,10},{26,18},{... | collective-permute-start | bytes 98312 | tf_op jit(solution)/shard_map/ppermute | solution.py:14
  8.2 70.8 %collective-permute-start.2 = (bf16[128,128]{1,0:T(8,128)(2,1)S(1)}, bf16[128,128]{1,0:T(8,128)(2,1)S(1)}, u32[]{:S(2)}, u32[]{:S(2)}) collective-permute-start(bf16[128,128]{1,0:T(8,128)(2,1)S(1)} %get-tuple-element.354), channel_id=1, source_target_pairs={{0,1},{1,2},{2,3},{3,4},{4,5},{5,6},{6,7},{8,9},{9,10},{10,11},{11... | collective-permute-start | bytes 98312 | tf_op jit(solution)/shard_map/ppermute | solution.py:14
  12.4 66.6 %collective-permute-start.3 = (bf16[128,128]{1,0:T(8,128)(2,1)S(1)}, bf16[128,128]{1,0:T(8,128)(2,1)S(1)}, u32[]{:S(2)}, u32[]{:S(2)}) collective-permute-start(bf16[128,128]{1,0:T(8,128)(2,1)S(1)} %get-tuple-element.353), channel_id=1, source_target_pairs={{1,0},{2,1},{3,2},{4,3},{5,4},{6,5},{7,6},{9,8},{10,9},{11,10},{12... | collective-permute-start | bytes 98312 | tf_op jit(solution)/shard_map/ppermute | solution.py:14
  15.2 62.7 %copy-start.13 = (f32[2,128]{1,0:T(2,128)S(1)}, f32[2,128]{1,0:T(2,128)}, u32[]{:S(2)}) copy-start(f32[2,128]{1,0:T(2,128)} %param.37) | copy-start | bytes 3076
  15.2 63.3 %copy-start.16 = (bf16[2,128,128]{2,1,0:T(8,128)(2,1)S(1)}, bf16[2,128,128]{2,1,0:T(8,128)(2,1)}, u32[]{:S(2)}) copy-start(bf16[2,128,128]{2,1,0:T(8,128)(2,1)} %param.34) | copy-start | bytes 196612
  77.3 1.5 copy-start.4
  77.3 1.5 copy-start.5
  129.9 1.7 copy-start.8
  129.9 1.7 copy-start.9
  131.4 0.7 copy-start.18
  131.5 4.0 %copy-start.17 = (bf16[2,128,128]{2,1,0:T(8,128)(2,1)S(1)}, bf16[2,128,128]{2,1,0:T(8,128)(2,1)}, u32[]{:S(2)}) copy-start(bf16[2,128,128]{2,1,0:T(8,128)(2,1)} %param.34) | copy-start | bytes 196612
  132.7 16.4 %copy-start.3 = (bf16[128,128]{1,0:T(8,128)(2,1)S(1)}, bf16[128,128]{1,0:T(8,128)(2,1)}, u32[]{:S(2)}) copy-start(bf16[128,128]{1,0:T(8,128)(2,1)} %get-tuple-element.643) | copy-start | bytes 98308
  132.8 11.9 %collective-permute-start.4 = (bf16[128,128]{0,1:T(8,128)(2,1)S(1)}, bf16[128,128]{0,1:T(8,128)(2,1)S(1)}, u32[]{:S(2)}, u32[]{:S(2)}) collective-permute-start(bf16[128,128]{0,1:T(8,128)(2,1)S(1)} %get-tuple-element.352), channel_id=1, source_target_pairs={{0,8},{8,16},{16,24},{1,9},{9,17},{17,25},{2,10},{10,18},{18,26},{... | collective-permute-start | bytes 98312 | tf_op jit(solution)/shard_map/ppermute | solution.py:14
  136.5 8.2 %collective-permute-start.5 = (bf16[128,128]{0,1:T(8,128)(2,1)S(1)}, bf16[128,128]{0,1:T(8,128)(2,1)S(1)}, u32[]{:S(2)}, u32[]{:S(2)}) collective-permute-start(bf16[128,128]{0,1:T(8,128)(2,1)S(1)} %get-tuple-element.351), channel_id=1, source_target_pairs={{8,0},{16,8},{24,16},{9,1},{17,9},{25,17},{10,2},{18,10},{26,18},{... | collective-permute-start | bytes 98312 | tf_op jit(solution)/shard_map/ppermute | solution.py:14
  139.1 5.7 %collective-permute-start.6 = (bf16[128,128]{0,1:T(8,128)(2,1)S(1)}, bf16[128,128]{0,1:T(8,128)(2,1)S(1)}, u32[]{:S(2)}, u32[]{:S(2)}) collective-permute-start(bf16[128,128]{0,1:T(8,128)(2,1)S(1)} %get-tuple-element.350), channel_id=1, source_target_pairs={{0,1},{1,2},{2,3},{3,4},{4,5},{5,6},{6,7},{8,9},{9,10},{10,11},{11... | collective-permute-start | bytes 98312 | tf_op jit(solution)/shard_map/ppermute | solution.py:14
  142.8 6.1 %collective-permute-start.7 = (bf16[128,128]{0,1:T(8,128)(2,1)S(1)}, bf16[128,128]{0,1:T(8,128)(2,1)S(1)}, u32[]{:S(2)}, u32[]{:S(2)}) collective-permute-start(bf16[128,128]{0,1:T(8,128)(2,1)S(1)} %get-tuple-element.349), channel_id=1, source_target_pairs={{1,0},{2,1},{3,2},{4,3},{5,4},{6,5},{7,6},{9,8},{10,9},{11,10},{12... | collective-permute-start | bytes 98312 | tf_op jit(solution)/shard_map/ppermute | solution.py:14
  149.1 49.1 %copy-start.14 = (f32[128]{0:T(128)S(1)}, f32[128]{0:T(128)}, u32[]{:S(2)}) copy-start(f32[128]{0:T(128)} %get-tuple-element.362) | copy-start | bytes 1540
  149.2 49.1 %copy-start.15 = (bf16[2,384,128]{2,1,0:T(8,128)(2,1)S(1)}, bf16[2,384,128]{2,1,0:T(8,128)(2,1)}, u32[]{:S(2)}) copy-start(bf16[2,384,128]{2,1,0:T(8,128)(2,1)} %param.33) | copy-start | bytes 589828
where the time goes:
time: 202 us; the launch traced here: 201 us
  matrix products  87.2 us (43%)
  blocking collectives  61.3 us (30%)
  starting transfers between devices  22.3 us (11%)
  local copies, waits for them, and re-layouts  19.7 us (10%)
  waiting for transfers between devices  4.14 us (2%)
  other arithmetic  3.71 us (2%)
    psum x1, blocking collectives, local(): total = lax.psum(local_sum, ('row', 'col'))  40.4 us
    dot_general x20, matrix products, lookup(): jnp.dot(picker, table, preferred_element_type=jnp.float32)  27 us
    dot_general x18, matrix products, norm_tail(): y_val = jnp.dot(hidden, w_out, preferred_element_type=jnp.float32) + b_out  26.1 us
    ppermute x8, starting transfers between devices, passed_along(): return lax.ppermute(value, axis, pairs)  22.3 us
    dot_general x16, matrix products, one_block(): jnp.dot(recv_hot, nodes, preferred_element_type=jnp.float32)  20.8 us
    all_gather x1, blocking collectives, local(): table = lax.all_gather(by_row, 'col', axis=1, tiled=True).reshape(-1, width)  12.8 us
    dot_general x16, matrix products, one_block(): lax.dot_general(recv_hot, fresh, (((0,), (0,)), ((), ())), preferred_elem...  12.3 us
    dynamic_slice x32, local copies, waits for them, and re-layouts, edge_and_sum(): summed, fresh = lax.scan(one_block, start, items)  8.37 us
  transfers between devices with their start and end apart: 8, of which 1 were waited for; matrix products, arithmetic and copies ran while one was open for 2% of the time, Pallas kernels for 0%

commit v1 on v0

--- a/solution.py
+++ b/solution.py
@@ -126,7 +126,8 @@
 ):
     width = node_latent.shape[1]
     local_sum = jnp.sum(node_latent.astype(jnp.float32), axis=0)
-    total = lax.psum(local_sum, ("row", "col"))
+    top = lax.psum(local_sum, "row")
+    total = lax.psum(top, "col")
     by_row = lax.all_gather(context_table[None], "row", axis=0, tiled=True)
     table = lax.all_gather(by_row, "col", axis=1, tiled=True).reshape(-1, width)
     node_count = node_latent.shape[0] * lax.axis_size("row") * lax.axis_size("col")

time: 202 us -> 183 us (0.906)
  blocking collectives: 61.3 us -> 42.2 us
    psum x1 -> x2, blocking collectives: 40.4 us -> 20.3 us  [the longest x1 13.1 us: local(): total = lax.psum(top, 'col')]
where the time goes in v1:
time: 183 us; the launch traced here: 182 us
  matrix products  87 us (48%)
  blocking collectives  42.2 us (23%)
  starting transfers between devices  22.6 us (12%)
  local copies, waits for them, and re-layouts  19.7 us (11%)
  waiting for transfers between devices  4.14 us (2%)
  other arithmetic  3.71 us (2%)
    dot_general x20, matrix products, lookup(): jnp.dot(picker, table, preferred_element_type=jnp.float32)  26.9 us
    dot_general x18, matrix products, norm_tail(): y_val = jnp.dot(hidden, w_out, preferred_element_type=jnp.float32) + b_out  26.1 us
    ppermute x8, starting transfers between devices, passed_along(): return lax.ppermute(value, axis, pairs)  22.6 us
    dot_general x16, matrix products, one_block(): jnp.dot(recv_hot, nodes, preferred_element_type=jnp.float32)  20.7 us
    psum x1, blocking collectives, local(): total = lax.psum(top, 'col')  13.1 us
    dot_general x16, matrix products, one_block(): lax.dot_general(recv_hot, fresh, (((0,), (0,)), ((), ())), preferred_elem...  12.3 us
    all_gather x1, blocking collectives, local(): table = lax.all_gather(by_row, 'col', axis=1, tiled=True).reshape(-1, width)  12 us
    all_gather x1, blocking collectives, local(): by_row = lax.all_gather(context_table[None], 'row', axis=0, tiled=True)  9.91 us
  transfers between devices with their start and end apart: 8, of which 1 were waited for; matrix products, arithmetic and copies ran while one was open for 2% of the time, Pallas kernels for 0%

profile of v1, /device:TPU:11, one launch (start us, length us, event | category | flops | bytes accessed | tf_op | source)
XLA Modules:
  0.0 181.8 jit_solution(10107419600586527363)
XLA Ops:
  0.7 1.5 fusion.61
  2.9 3.2 %collective-permute-start = (bf16[128,128]{1,0:T(8,128)(2,1)}, bf16[128,128]{1,0:T(8,128)(2,1)S(1)}, u32[]{:S(2)}, u32[]{:S(2)}) collective-permute-start(bf16[128,128]{1,0:T(8,128)(2,1)} %get-tuple-element.356), channel_id=1, source_target_pairs={{0,8},{8,16},{16,24},{1,9},{9,17},{17,25},{2,10},{10,18},{18,26},{... | collective-permute-start | bytes 98312 | tf_op jit(solution)/shard_map/ppermute | solution.py:14
  6.1 2.1 %collective-permute-start.1 = (bf16[128,128]{1,0:T(8,128)(2,1)}, bf16[128,128]{1,0:T(8,128)(2,1)S(1)}, u32[]{:S(2)}, u32[]{:S(2)}) collective-permute-start(bf16[128,128]{1,0:T(8,128)(2,1)} %get-tuple-element.355), channel_id=1, source_target_pairs={{8,0},{16,8},{24,16},{9,1},{17,9},{25,17},{10,2},{18,10},{26,18},{... | collective-permute-start | bytes 98312 | tf_op jit(solution)/shard_map/ppermute | solution.py:14
  8.2 4.2 %collective-permute-start.2 = (bf16[128,128]{1,0:T(8,128)(2,1)S(1)}, bf16[128,128]{1,0:T(8,128)(2,1)S(1)}, u32[]{:S(2)}, u32[]{:S(2)}) collective-permute-start(bf16[128,128]{1,0:T(8,128)(2,1)S(1)} %get-tuple-element.354), channel_id=1, source_target_pairs={{0,1},{1,2},{2,3},{3,4},{4,5},{5,6},{6,7},{8,9},{9,10},{10,11},{11... | collective-permute-start | bytes 98312 | tf_op jit(solution)/shard_map/ppermute | solution.py:14
  12.4 1.9 %collective-permute-start.3 = (bf16[128,128]{1,0:T(8,128)(2,1)S(1)}, bf16[128,128]{1,0:T(8,128)(2,1)S(1)}, u32[]{:S(2)}, u32[]{:S(2)}) collective-permute-start(bf16[128,128]{1,0:T(8,128)(2,1)S(1)} %get-tuple-element.353), channel_id=1, source_target_pairs={{1,0},{2,1},{3,2},{4,3},{5,4},{6,5},{7,6},{9,8},{10,9},{11,10},{12... | collective-permute-start | bytes 98312 | tf_op jit(solution)/shard_map/ppermute | solution.py:14
  15.3 7.2 %psum.14 = f32[128]{0:T(128)S(1)} all-reduce(f32[128]{0:T(128)S(1)} %convert_reduce_fusion), channel_id=1, replica_groups=mesh['row'=4,'col'=8] {'row'}, use_global_device_ids=true, to_apply=%region_7.8 | all-reduce | flops 128 | bytes 1024 | tf_op jit(solution)/shard_map/psum | solution.py:129
  22.5 13.1 %psum.15 = f32[128]{0:T(128)S(1)} all-reduce(f32[128]{0:T(128)S(1)} %psum.14), channel_id=1, replica_groups=mesh['row'=4,'col'=8] {'col'}, use_global_device_ids=true, to_apply=%region_8.9 | all-reduce | flops 128 | bytes 1024 | tf_op jit(solution)/shard_map/psum | solution.py:130
  36.2 9.9 %all-gather = bf16[32,128]{1,0:T(8,128)(2,1)S(1)} all-gather(bf16[8,128]{1,0:T(8,128)(2,1)S(1)} %copy-done.10), channel_id=2, replica_groups=mesh['row'=4,'col'=8] {'row'}, dimensions={0}, use_global_device_ids=true | all-gather | bytes 10240 | tf_op jit(solution)/shard_map/all_gather | solution.py:131
  46.2 12.0 %all_gather.7 = bf16[4,64,128]{2,1,0:T(8,128)(2,1)S(1)} all-gather(bf16[4,8,128]{2,1,0:T(8,128)(2,1)S(1)} %bitcast.189), channel_id=1, replica_groups=mesh['row'=4,'col'=8] {'col'}, dimensions={1}, use_global_device_ids=true | all-gather | bytes 73728 | tf_op jit(solution)/shard_map/all_gather | solution.py:132
  59.9 50.7 %while.37 = (s32[]{:T(128)}, f32[1024,128]{1,0:T(8,128)S(1)}, bf16[8,512,128]{1,2,0:T(8,128)(2,1)S(1)}, s32[8,512]{1,0:T(8,128)S(1)}, bf16[8,512,128]{2,1,0:T(8,...) while((s32[]{:T(128)}, f32[1024,128]{1,0:T(8,128)S(1)}, ...), condition=%wide.region_3.4_spmd.clone, body=%wide.region_0.3_spmd.clone.sunk | while | flops 541786624 | bytes 4363419 | solution.py:73
  61.2 1.5 fusion.176
  67.5 1.5 fusion.176
  73.8 1.5 fusion.176
  80.2 1.5 fusion.176
  86.5 1.5 fusion.176
  92.8 1.5 fusion.176
  105.5 1.5 fusion.176
  110.7 1.5 fusion.125
  113.6 4.0 %collective-permute-start.4 = (bf16[128,128]{0,1:T(8,128)(2,1)S(1)}, bf16[128,128]{0,1:T(8,128)(2,1)S(1)}, u32[]{:S(2)}, u32[]{:S(2)}) collective-permute-start(bf16[128,128]{0,1:T(8,128)(2,1)S(1)} %get-tuple-element.352), channel_id=1, source_target_pairs={{0,8},{8,16},{16,24},{1,9},{9,17},{17,25},{2,10},{10,18},{18,26},{... | collective-permute-start | bytes 98312 | tf_op jit(solution)/shard_map/ppermute | solution.py:14
  118.5 1.9 %collective-permute-start.5 = (bf16[128,128]{0,1:T(8,128)(2,1)S(1)}, bf16[128,128]{0,1:T(8,128)(2,1)S(1)}, u32[]{:S(2)}, u32[]{:S(2)}) collective-permute-start(bf16[128,128]{0,1:T(8,128)(2,1)S(1)} %get-tuple-element.351), channel_id=1, source_target_pairs={{8,0},{16,8},{24,16},{9,1},{17,9},{25,17},{10,2},{18,10},{26,18},{... | collective-permute-start | bytes 98312 | tf_op jit(solution)/shard_map/ppermute | solution.py:14
  120.5 3.4 %collective-permute-start.6 = (bf16[128,128]{0,1:T(8,128)(2,1)S(1)}, bf16[128,128]{0,1:T(8,128)(2,1)S(1)}, u32[]{:S(2)}, u32[]{:S(2)}) collective-permute-start(bf16[128,128]{0,1:T(8,128)(2,1)S(1)} %get-tuple-element.350), channel_id=1, source_target_pairs={{0,1},{1,2},{2,3},{3,4},{4,5},{5,6},{6,7},{8,9},{9,10},{10,11},{11... | collective-permute-start | bytes 98312 | tf_op jit(solution)/shard_map/ppermute | solution.py:14
  123.9 1.9 %collective-permute-start.7 = (bf16[128,128]{0,1:T(8,128)(2,1)S(1)}, bf16[128,128]{0,1:T(8,128)(2,1)S(1)}, u32[]{:S(2)}, u32[]{:S(2)}) collective-permute-start(bf16[128,128]{0,1:T(8,128)(2,1)S(1)} %get-tuple-element.349), channel_id=1, source_target_pairs={{1,0},{2,1},{3,2},{4,3},{5,4},{6,5},{7,6},{9,8},{10,9},{11,10},{12... | collective-permute-start | bytes 98312 | tf_op jit(solution)/shard_map/ppermute | solution.py:14
  125.9 4.1 %collective-permute-done.7 = bf16[128,128]{0,1:T(8,128)(2,1)S(1)} collective-permute-done((bf16[128,128]{0,1:T(8,128)(2,1)S(1)}, bf16[128,128]{0,1:T(8,128)(2,1)S(1)}, u32[]{:S(2)}, u32[]{:S(2)}) %collective-permute-start.7) | collective-permute-done | bytes 32800 | tf_op jit(solution)/shard_map/ppermute | solution.py:14
  130.3 48.8 %while.38 = (s32[]{:T(128)}, f32[1024,128]{1,0:T(8,128)S(1)}, bf16[8,512,128]{2,1,0:T(8,128)(2,1)}, s32[8,512]{1,0:T(8,128)S(1)}, bf16[8,512,128]{1,2,0:T(8,128)...) while((s32[]{:T(128)}, f32[1024,128]{1,0:T(8,128)S(1)}, ...), condition=%wide.region_14.15_spmd.clone, body=%wide.region_11.14_spmd.clone.sunk | while | flops 541786624 | bytes 4495003 | solution.py:73
  131.6 1.5 fusion.186
  137.7 1.5 fusion.186
  143.8 1.5 fusion.186
  149.9 1.5 fusion.186
  156.0 1.5 fusion.186
  162.1 1.5 fusion.186
  168.2 1.5 fusion.186
  174.3 1.5 fusion.186
  (282 shorter events, 85.4 us)
Async XLA Ops:
  0.6 13.7 %copy-start = (bf16[1024,128]{1,0:T(8,128)(2,1)S(1)}, bf16[1024,128]{1,0:T(8,128)(2,1)}, u32[]{:S(2)}) copy-start(bf16[1024,128]{1,0:T(8,128)(2,1)} %param.22) | copy-start | bytes 786436
  0.6 13.9 %copy-start.1 = (bf16[2,384,128]{2,1,0:T(8,128)(2,1)S(1)}, bf16[2,384,128]{2,1,0:T(8,128)(2,1)}, u32[]{:S(2)}) copy-start(bf16[2,384,128]{2,1,0:T(8,128)(2,1)} %param.29) | copy-start | bytes 589828
  0.7 13.9 %copy-start.2 = (bf16[2,128,128]{2,1,0:T(8,128)(2,1)S(1)}, bf16[2,128,128]{2,1,0:T(8,128)(2,1)}, u32[]{:S(2)}) copy-start(bf16[2,128,128]{2,1,0:T(8,128)(2,1)} %param.30) | copy-start | bytes 196612
  0.7 14.5 %copy-start.7 = (f32[2,3,128]{2,0,1:T(2,128)S(1)}, f32[2,3,128]{2,0,1:T(2,128)}, u32[]{:S(2)}) copy-start(f32[2,3,128]{2,0,1:T(2,128)} %param.31) | copy-start | bytes 9220
  0.7 14.5 %copy-start.12 = (f32[2,128]{1,0:T(2,128)S(1)}, f32[2,128]{1,0:T(2,128)}, u32[]{:S(2)}) copy-start(f32[2,128]{1,0:T(2,128)} %param.32) | copy-start | bytes 3076
  2.2 33.4 %copy-start.11 = (f32[2,3,128]{2,0,1:T(2,128)S(1)}, f32[2,3,128]{2,0,1:T(2,128)}, u32[]{:S(2)}) copy-start(f32[2,3,128]{2,0,1:T(2,128)} %param.36) | copy-start | bytes 9220
  2.2 34.0 %copy-start.10 = (bf16[8,128]{1,0:T(8,128)(2,1)S(1)}, bf16[8,128]{1,0:T(8,128)(2,1)}, u32[]{:S(2)}) copy-start(bf16[8,128]{1,0:T(8,128)(2,1)} %param.27) | copy-start | bytes 6148
  2.2 55.9 %copy-start.6 = (s32[1024]{0:T(1024)S(1)}, s32[1024]{0:T(1024)}, u32[]{:S(2)}) copy-start(s32[1024]{0:T(1024)} %param.28) | copy-start | bytes 12292
  2.9 56.9 %collective-permute-start = (bf16[128,128]{1,0:T(8,128)(2,1)}, bf16[128,128]{1,0:T(8,128)(2,1)S(1)}, u32[]{:S(2)}, u32[]{:S(2)}) collective-permute-start(bf16[128,128]{1,0:T(8,128)(2,1)} %get-tuple-element.356), channel_id=1, source_target_pairs={{0,8},{8,16},{16,24},{1,9},{9,17},{17,25},{2,10},{10,18},{18,26},{... | collective-permute-start | bytes 98312 | tf_op jit(solution)/shard_map/ppermute | solution.py:14
  6.1 53.7 %collective-permute-start.1 = (bf16[128,128]{1,0:T(8,128)(2,1)}, bf16[128,128]{1,0:T(8,128)(2,1)S(1)}, u32[]{:S(2)}, u32[]{:S(2)}) collective-permute-start(bf16[128,128]{1,0:T(8,128)(2,1)} %get-tuple-element.355), channel_id=1, source_target_pairs={{8,0},{16,8},{24,16},{9,1},{17,9},{25,17},{10,2},{18,10},{26,18},{... | collective-permute-start | bytes 98312 | tf_op jit(solution)/shard_map/ppermute | solution.py:14
  8.2 51.6 %collective-permute-start.2 = (bf16[128,128]{1,0:T(8,128)(2,1)S(1)}, bf16[128,128]{1,0:T(8,128)(2,1)S(1)}, u32[]{:S(2)}, u32[]{:S(2)}) collective-permute-start(bf16[128,128]{1,0:T(8,128)(2,1)S(1)} %get-tuple-element.354), channel_id=1, source_target_pairs={{0,1},{1,2},{2,3},{3,4},{4,5},{5,6},{6,7},{8,9},{9,10},{10,11},{11... | collective-permute-start | bytes 98312 | tf_op jit(solution)/shard_map/ppermute | solution.py:14
  12.4 47.4 %collective-permute-start.3 = (bf16[128,128]{1,0:T(8,128)(2,1)S(1)}, bf16[128,128]{1,0:T(8,128)(2,1)S(1)}, u32[]{:S(2)}, u32[]{:S(2)}) collective-permute-start(bf16[128,128]{1,0:T(8,128)(2,1)S(1)} %get-tuple-element.353), channel_id=1, source_target_pairs={{1,0},{2,1},{3,2},{4,3},{5,4},{6,5},{7,6},{9,8},{10,9},{11,10},{12... | collective-permute-start | bytes 98312 | tf_op jit(solution)/shard_map/ppermute | solution.py:14
  15.2 43.6 %copy-start.13 = (f32[2,128]{1,0:T(2,128)S(1)}, f32[2,128]{1,0:T(2,128)}, u32[]{:S(2)}) copy-start(f32[2,128]{1,0:T(2,128)} %param.37) | copy-start | bytes 3076
  15.2 44.1 %copy-start.16 = (bf16[2,128,128]{2,1,0:T(8,128)(2,1)S(1)}, bf16[2,128,128]{2,1,0:T(8,128)(2,1)}, u32[]{:S(2)}) copy-start(bf16[2,128,128]{2,1,0:T(8,128)(2,1)} %param.34) | copy-start | bytes 196612
  58.1 1.4 copy-start.4
  58.1 1.4 copy-start.5
  110.7 1.7 copy-start.8
  110.7 1.7 copy-start.9
  112.2 0.7 copy-start.18
  112.3 5.2 %copy-start.17 = (bf16[2,128,128]{2,1,0:T(8,128)(2,1)S(1)}, bf16[2,128,128]{2,1,0:T(8,128)(2,1)}, u32[]{:S(2)}) copy-start(bf16[2,128,128]{2,1,0:T(8,128)(2,1)} %param.34) | copy-start | bytes 196612
  113.5 16.7 %copy-start.3 = (bf16[128,128]{1,0:T(8,128)(2,1)S(1)}, bf16[128,128]{1,0:T(8,128)(2,1)}, u32[]{:S(2)}) copy-start(bf16[128,128]{1,0:T(8,128)(2,1)} %get-tuple-element.643) | copy-start | bytes 98308
  113.6 12.2 %collective-permute-start.4 = (bf16[128,128]{0,1:T(8,128)(2,1)S(1)}, bf16[128,128]{0,1:T(8,128)(2,1)S(1)}, u32[]{:S(2)}, u32[]{:S(2)}) collective-permute-start(bf16[128,128]{0,1:T(8,128)(2,1)S(1)} %get-tuple-element.352), channel_id=1, source_target_pairs={{0,8},{8,16},{16,24},{1,9},{9,17},{17,25},{2,10},{10,18},{18,26},{... | collective-permute-start | bytes 98312 | tf_op jit(solution)/shard_map/ppermute | solution.py:14
  118.5 7.3 %collective-permute-start.5 = (bf16[128,128]{0,1:T(8,128)(2,1)S(1)}, bf16[128,128]{0,1:T(8,128)(2,1)S(1)}, u32[]{:S(2)}, u32[]{:S(2)}) collective-permute-start(bf16[128,128]{0,1:T(8,128)(2,1)S(1)} %get-tuple-element.351), channel_id=1, source_target_pairs={{8,0},{16,8},{24,16},{9,1},{17,9},{25,17},{10,2},{18,10},{26,18},{... | collective-permute-start | bytes 98312 | tf_op jit(solution)/shard_map/ppermute | solution.py:14
  120.5 5.4 %collective-permute-start.6 = (bf16[128,128]{0,1:T(8,128)(2,1)S(1)}, bf16[128,128]{0,1:T(8,128)(2,1)S(1)}, u32[]{:S(2)}, u32[]{:S(2)}) collective-permute-start(bf16[128,128]{0,1:T(8,128)(2,1)S(1)} %get-tuple-element.350), channel_id=1, source_target_pairs={{0,1},{1,2},{2,3},{3,4},{4,5},{5,6},{6,7},{8,9},{9,10},{10,11},{11... | collective-permute-start | bytes 98312 | tf_op jit(solution)/shard_map/ppermute | solution.py:14
  123.9 6.1 %collective-permute-start.7 = (bf16[128,128]{0,1:T(8,128)(2,1)S(1)}, bf16[128,128]{0,1:T(8,128)(2,1)S(1)}, u32[]{:S(2)}, u32[]{:S(2)}) collective-permute-start(bf16[128,128]{0,1:T(8,128)(2,1)S(1)} %get-tuple-element.349), channel_id=1, source_target_pairs={{1,0},{2,1},{3,2},{4,3},{5,4},{6,5},{7,6},{9,8},{10,9},{11,10},{12... | collective-permute-start | bytes 98312 | tf_op jit(solution)/shard_map/ppermute | solution.py:14
  130.2 49.0 %copy-start.14 = (f32[128]{0:T(128)S(1)}, f32[128]{0:T(128)}, u32[]{:S(2)}) copy-start(f32[128]{0:T(128)} %get-tuple-element.362) | copy-start | bytes 1540
  130.3 49.0 %copy-start.15 = (bf16[2,384,128]{2,1,0:T(8,128)(2,1)S(1)}, bf16[2,384,128]{2,1,0:T(8,128)(2,1)}, u32[]{:S(2)}) copy-start(bf16[2,384,128]{2,1,0:T(8,128)(2,1)} %param.33) | copy-start | bytes 589828
